TPU v7x, 32 devices: a whole 2x2x4 slice. The times are simulated.
32 devices in a mesh: station: 16 (over z, x, core), chan: 2 (over y).
Axes of the slice: x: 2, y: 2, z: 4, core: 2. Of those that a mesh axis runs over, the one named last changes fastest.
Arguments:
- samples: float32 [2, 16, 256, 128, 256], P(None, 'station', 'chan'), may hold values from -6 to 6
- weights: float32 [2, 16, 32, 256, 256], P(None, 'station', None, 'chan'), may hold values from -6 to 6
- antenna_flags: int32 [16, 256], P('station', 'chan'), may hold values from 0 to 1, as said below
- subband_table: int32 [256], replicated, may hold values from 0 to 255, each once
Outputs:
- visibilities: float32 [256, 2, 16, 32, 16], P('chan', None, 'station')
Inputs may be any that keep to these rules, and one draw needn't show every extreme that they name: `antenna_flags`: every station has at least 32 antennas with flag 1. `subband_table`: a permutation of 0 to 255.
All inputs are finite; a program needn't handle non-finite values.
Results may differ from a plain program's by a relative error of at most 0.0019.
Values may be sent and summed in bfloat16 or wider, within the bound.
A program may use at most 192 MiB of HBM per device.

v0:
```python
import functools

import jax
import jax.numpy as jnp
from jax import lax
from jax.experimental import pallas as pl
from jax.experimental.pallas import tpu as pltpu
from jax.sharding import PartitionSpec as P

LANES = 128
ANTENNAS_PER_STEP = 16
UNROLL = 4


def split(value):
    high = value.astype(jnp.bfloat16)
    low = (value - high.astype(jnp.float32)).astype(jnp.bfloat16)
    return high, low


def beam_kernel(table_ref, x_ref, w_ref, usable_ref, sent_ref, own_ref, slot_ref, x_rows, w_rows, *, antennas, beams):
    block, step = pl.program_id(0), pl.program_id(1)
    mine = lax.axis_index("chan")
    subbands = sent_ref.shape[0]
    kept = own_ref.shape[0] - 1
    x_stride = x_rows.shape[0] // LANES
    w_stride = w_rows.shape[0] // LANES
    x_step = x_ref.shape[2]
    w_step = w_ref.shape[2]

    @pl.when((block == 0) & (step == 0))
    def _():
        @pl.loop(0, subbands)
        def _(slot):
            slot_ref[table_ref[slot]] = slot

    for part in range(2):
        for a in range(x_step):
            row = part * antennas + step * x_step + a
            x_rows[pl.ds(row, LANES, stride=x_stride), :] = x_ref[part, 0, a].T
        for b in range(w_step):
            tile = w_ref[part, 0, b]
            if antennas < LANES:
                tile = jnp.concatenate([tile, jnp.zeros((LANES - antennas, LANES), jnp.float32)], axis=0)
            row = part * beams + step * w_step + b
            w_rows[pl.ds(row, LANES, stride=w_stride), :] = tile.T

    @pl.when(step == pl.num_programs(1) - 1)
    def _():
        usable = usable_ref[...]

        def one(f):
            x = x_rows[pl.ds(pl.multiple_of(f * x_stride, 8), 2 * antennas), :]
            w = w_rows[pl.ds(pl.multiple_of(f * w_stride, 8), 2 * beams), :][:, :antennas] * usable
            w_re, w_im = w[:beams], w[beams:]
            steer = jnp.concatenate(
                [jnp.concatenate([w_re, -w_im], axis=1), jnp.concatenate([w_im, w_re], axis=1)], axis=0
            )
            x_pair = jnp.concatenate(split(x), axis=1)
            w_pair = jnp.concatenate(split(steer), axis=0)
            grid = jnp.dot(w_pair, x_pair, preferred_element_type=jnp.float32)
            rows, cols = 2 * beams, x.shape[1]
            total = grid[:rows, :cols] + (grid[rows:, :cols] + grid[:rows, cols:] + grid[rows:, cols:])
            slot = slot_ref[block * LANES + f]
            sent_ref[slot] = total.astype(jnp.bfloat16)
            local = slot - mine * kept
            own_ref[jnp.where((local >= 0) & (local < kept), local, kept)] = total

        @pl.loop(0, LANES // UNROLL)
        def _(group):
            for u in range(UNROLL):
                one(group * UNROLL + u)


def beam_partials(samples, weights, usable, table, groups):
    _, _, antennas, times, subbands = samples.shape
    beams = weights.shape[2]
    steps = antennas // ANTENNAS_PER_STEP
    w_step = beams // steps
    grid_spec = pltpu.PrefetchScalarGridSpec(
        num_scalar_prefetch=1,
        grid=(subbands // LANES, steps),
        in_specs=[
            pl.BlockSpec((2, 1, ANTENNAS_PER_STEP, times, LANES), lambda f, s, *_: (0, 0, s, 0, f)),
            pl.BlockSpec((2, 1, w_step, antennas, LANES), lambda f, s, *_: (0, 0, s, 0, f)),
            pl.BlockSpec((1, antennas), lambda f, s, *_: (0, 0)),
        ],
        out_specs=[
            pl.BlockSpec((subbands, 2 * beams, times), lambda f, s, *_: (0, 0, 0)),
            pl.BlockSpec((subbands // groups + 1, 2 * beams, times), lambda f, s, *_: (0, 0, 0)),
        ],
        scratch_shapes=[
            pltpu.SMEM((subbands,), jnp.int32),
            pltpu.VMEM((LANES * (2 * antennas + 8), times), jnp.float32),
            pltpu.VMEM((LANES * (2 * beams + 8), LANES), jnp.float32),
        ],
    )
    return pl.pallas_call(
        functools.partial(beam_kernel, antennas=antennas, beams=beams),
        grid_spec=grid_spec,
        out_shape=[
            jax.ShapeDtypeStruct((subbands, 2 * beams, times), jnp.bfloat16),
            jax.ShapeDtypeStruct((subbands // groups + 1, 2 * beams, times), jnp.float32),
        ],
        compiler_params=pltpu.CompilerParams(
            dimension_semantics=("arbitrary", "arbitrary"), vmem_limit_bytes=60 * 1024 * 1024
        ),
    )(table, samples, weights, usable)


def on_device(samples, weights, antenna_flags, subband_table):
    usable = antenna_flags.astype(jnp.float32)
    usable_count = lax.psum(jnp.sum(usable, axis=1), "chan")
    gain_scale = lax.rsqrt(usable_count)
    groups = lax.axis_size("chan")
    mine = lax.axis_index("chan")
    beams, times = weights.shape[2], samples.shape[3]
    sent, own = beam_partials(samples, weights, usable, subband_table, groups)
    sent = sent.reshape(groups, -1, 2, beams, times)
    arrived = lax.all_to_all(sent, "chan", 0, 0)
    own = own[:-1].reshape(-1, 2, beams, times)
    is_mine = (jnp.arange(groups) == mine)[:, None, None, None, None]
    beam_sum = own + jnp.sum(jnp.where(is_mine, 0.0, arrived.astype(jnp.float32)), axis=0)
    beam_data = (beam_sum * gain_scale).astype(jnp.bfloat16)
    stations = lax.axis_size("station")
    spread = beam_data.reshape(stations, -1, *beam_data.shape[1:])
    gathered = lax.all_to_all(spread, "station", 0, 0)
    swapped = jnp.stack([gathered[:, :, 1], -gathered[:, :, 0]], axis=2)
    stacked = jnp.stack([gathered, swapped], axis=0)
    pairs = jnp.einsum("osfcbt,rfcbt->sfobr", stacked, gathered, preferred_element_type=jnp.float32)
    returned = lax.all_to_all(pairs, "station", 0, 0)
    return returned.reshape(-1, *returned.shape[2:])[:, :, None]


def solution(mesh):
    in_specs = (
        P(None, "station", "chan", None, None),
        P(None, "station", None, "chan", None),
        P("station", "chan"),
        P(),
    )
    out_specs = P("chan", None, "station", None, None)
    return jax.shard_map(
        on_device, mesh=mesh, in_specs=in_specs, out_specs=out_specs, check_vma=False
    )
```

profile of v0, /device:TPU:0, one launch (start us, length us, event | category | flops | bytes accessed | tf_op | source)
XLA Modules:
  0.0 203.6 jit_solution(13777267502648543792)
XLA Ops:
  0.0 1.2 convert_element_type.10.usable_ref
  1.2 41.8 %shard_map.46 = (bf16[256,64,128]{2,1,0:T(8,128)(2,1)}, f32[129,64,128]{2,1,0:T(8,128)}) custom-call(s32[256]{0:T(256)} %table_ref.1, f32[2,1,128,128,256]{4,3,2,1,0:T(8,128)} %x_ref.1, f32[2,1,32,128,256]{4,3,2,1,0:T(8,128)} %w_ref.1, f32[1,128]{1,0:T(1,128)} %convert_element_type.10.usable_ref), custom_call_target="tpu_custom_call" | custom-call | tf_op jit(solution)/shard_map/pallas_call | solution.py:98
  43.0 0.0 copy-start.1
  43.0 5.7 %all-to-all-start = ((bf16[2,128,2,32,128]{4,3,2,1,0:T(8,128)(2,1)}), bf16[2,128,2,32,128]{4,3,2,1,0:T(8,128)(2,1)}, u32[]{:S(2)}, u32[]{:S(2)}) async-start(bf16[2,128,2,32,128]{4,3,2,1,0:T(8,128)(2,1)} %bitcast.25), calls=%async_computation | async-start | bytes 8388608 | tf_op jit(solution)/shard_map/all_to_all | solution.py:120
  48.7 0.0 copy-done.1
  48.7 0.6 convert_reduce_fusion
  49.3 48.9 %psum.7 = f32[1]{0:T(128)} all-reduce(f32[1]{0:T(128)} %bitcast.3), channel_id=1, replica_groups=mesh['station'=16,'chan'=2] {'chan'}, use_global_device_ids=true, to_apply=%region_2.3 | all-reduce | flops 1 | bytes 8 | tf_op jit(solution)/shard_map/psum | solution.py:113
  98.2 4.7 %slice.9 = f32[128,64,128]{2,1,0:T(8,128)} slice(f32[129,64,128]{2,1,0:T(8,128)} %get-tuple-element.7), slice={[0:128], [0:64], [0:128]} | slice | bytes 8388608 | tf_op jit(solution)/shard_map/slice | solution.py:121
  103.6 0.0 all-to-all-done
  103.6 0.0 copy-start
  103.6 4.3 %select_reduce_fusion = f32[128,2,32,128]{3,2,1,0:T(8,128)S(1)} fusion(bf16[2,128,2,32,128]{4,3,2,1,0:T(8,128)(2,1)} %all-to-all-done, pred[2]{0:T(512)(128)(4,1)S(1)} %iota_compare_fusion), kind=kLoop, calls=%fused_computation | loop fusion | flops 5242880 | bytes 8388610 | tf_op jit(solution)/shard_map/reduce_sum | solution.py:123
  108.0 0.0 copy-done
  108.0 1.1 multiply_convert_fusion
  109.1 2.4 %copy.12 = bf16[16,8,2,32,128]{4,2,3,1,0:T(2,128)(2,1)S(1)} copy(bf16[16,8,2,32,128]{4,3,2,1,0:T(8,128)(2,1)S(1)} %multiply_convert_fusion) | data formatting | bytes 4194304 | tf_op jit(solution)/shard_map/convert_element_type | solution.py:124
  111.5 53.1 %all_to_all.15 = bf16[16,8,2,32,128]{4,2,3,1,0:T(2,128)(2,1)S(1)} all-to-all(bf16[16,8,2,32,128]{4,2,3,1,0:T(2,128)(2,1)S(1)} %copy.12), channel_id=1, replica_groups=mesh['station'=16,'chan'=2] {'station'}, dimensions={0} | all-to-all | bytes 4194304 | tf_op jit(solution)/shard_map/all_to_all | solution.py:127
  164.6 2.5 %copy.27 = bf16[16,8,2,32,128]{4,0,2,3,1:T(8,128)(2,1)S(1)} copy(bf16[16,8,2,32,128]{4,2,3,1,0:T(2,128)(2,1)S(1)} %all_to_all.15) | data formatting | bytes 4194304 | tf_op jit(solution)/shard_map/all_to_all | solution.py:127
  167.1 0.2 fusion.9
  167.3 0.2 maximum_bitcast_fusion
  167.5 6.5 %fusion.4 = f32[16,8,2,32,16]{0,4,2,3,1:T(8,128)} fusion(bf16[1,16,8,2,32,128]{5,1,3,0,4,2:T(8,128)(2,1)S(1)} %maximum_bitcast_fusion, bf16[1,16,8,2,32,128]{5,1,3,0,4,2:T(8,128)(2,1)S(1)} %bitcast.20, bf16[16,8,2,32,128,1]{4,2,3,1,0,5:T(2,128)(2,1)S(1)} %bitcast.19), kind=kOutput, calls=%fused_computation.6 | convolution fusion | flops 75497472 | bytes 6815744 | tf_op jit(solution)/shard_map/osfcbt,rfcbt->sfobr/dot_general | solution.py:130
  173.9 4.3 %copy.17 = f32[16,8,2,32,16]{3,4,2,1,0:T(8,128)S(1)} copy(f32[16,8,2,32,16]{0,4,2,3,1:T(8,128)} %fusion.4) | data formatting | bytes 1048576 | tf_op jit(solution)/shard_map/osfcbt,rfcbt->sfobr/transpose | solution.py:130
  178.2 0.9 reshape.19
  179.1 19.2 %all_to_all.16 = f32[16,1,8192]{2,1,0:T(1,128)S(1)} all-to-all(f32[16,1,8192]{2,1,0:T(1,128)S(1)} %reshape.19), channel_id=1, replica_groups=mesh['station'=16,'chan'=2] {'station'}, dimensions={0} | all-to-all | bytes 1048576 | tf_op jit(solution)/shard_map/all_to_all | solution.py:131
  198.4 0.5 broadcast.5
  198.9 1.9 reduce.1
  200.8 0.7 reshape.20
  201.5 2.2 %copy.18 = f32[128,2,1,32,16]{0,4,3,2,1:T(8,128)} copy(f32[128,2,1,32,16]{3,4,1,0,2:T(8,128)S(1)} %bitcast.24) | data formatting | bytes 1048576 | tf_op jit(solution)/shard_map/broadcast_in_dim;reshape | solution.py:132
  (1 shorter events, 0.0 us)
Async XLA Ops:
  43.0 5.7 %copy-start.1 = (s32[1,128]{1,0:T(1,128)S(1)}, s32[1,128]{1,0:T(1,128)}, u32[]{:S(2)}) copy-start(s32[1,128]{1,0:T(1,128)} %param.6) | copy-start | bytes 1540
  43.0 60.6 %all-to-all-start = ((bf16[2,128,2,32,128]{4,3,2,1,0:T(8,128)(2,1)}), bf16[2,128,2,32,128]{4,3,2,1,0:T(8,128)(2,1)}, u32[]{:S(2)}, u32[]{:S(2)}) async-start(bf16[2,128,2,32,128]{4,3,2,1,0:T(8,128)(2,1)} %bitcast.25), calls=%async_computation | async-start | bytes 8388608 | tf_op jit(solution)/shard_map/all_to_all | solution.py:120
  103.6 4.3 %copy-start = (f32[128,64,128]{2,1,0:T(8,128)S(1)}, f32[128,64,128]{2,1,0:T(8,128)}, u32[]{:S(2)}) copy-start(f32[128,64,128]{2,1,0:T(8,128)} %slice.9) | copy-start | bytes 12582916
where the time goes:
time: 204 us
  blocking collectives  121 us (59%)
  Pallas kernels  41.8 us (20%)
  local copies, waits for them, and re-layouts  18.2 us (9%)
  other arithmetic  9.48 us (5%)
  matrix products  6.47 us (3%)
  starting transfers between devices  5.72 us (3%)
    all_to_all x1, blocking collectives, on_device(): gathered = lax.all_to_all(spread, 'station', 0, 0)  53.1 us
    psum x1, blocking collectives, on_device(): usable_count = lax.psum(jnp.sum(usable, axis=1), 'chan')  48.9 us
    pallas_call x1, Pallas kernels, beam_partials(): pl.pallas_call(functools.partial(beam_kernel, antennas=antennas, beams=be...  41.8 us
    all_to_all x1, blocking collectives, on_device(): returned = lax.all_to_all(pairs, 'station', 0, 0)  19.2 us
    dot_general x1, matrix products, on_device(): jnp.einsum('osfcbt,rfcbt->sfobr', stacked, gathered, preferred_element_ty...  6.47 us
    all_to_all x1, starting transfers between devices, on_device(): arrived = lax.all_to_all(sent, 'chan', 0, 0)  5.72 us
    slice x1, local copies, waits for them, and re-layouts, on_device(): own = own[:-1].reshape(-1, 2, beams, times)  4.72 us
    reduce_sum x1, other arithmetic, on_device(): jnp.sum(jnp.where(is_mine, 0.0, arrived.astype(jnp.float32)), axis=0)  4.33 us
  transfers between devices with their start and end apart: 1, of which 0 were waited for; matrix products, arithmetic and copies ran while one was open for 3% of the time, Pallas kernels for 0%

commit v1 on v0

--- a/solution.py
+++ b/solution.py
@@ -10,6 +10,7 @@
 LANES = 128
 ANTENNAS_PER_STEP = 16
 UNROLL = 4
+STATIONS_PER_STEP = 4
 
 
 def split(value):
@@ -108,28 +109,242 @@
     )(table, samples, weights, usable)
 
 
+def exchange_kernel(
+    sent_ref, own_hbm, count_ref, out_ref,
+    own, arrived, outgoing, gathered, sums, returned, counts,
+    own_sem, count_send, count_recv, chan_send, chan_recv, beam_send, beam_recv, back_send, back_recv,
+):
+    groups, stations = lax.axis_size("chan"), lax.axis_size("station")
+    mine, me = lax.axis_index("chan"), lax.axis_index("station")
+    phases, _, depth, rows, times = gathered.shape
+    beams = rows // 2
+    kept = own.shape[0]
+    share = phases * depth
+    wide = min(STATIONS_PER_STEP, stations)
+    pieces = stations // wide
+
+    def target(k):
+        return lax.rem(me + stations // 2 + ((k + 1) // 2) * (1 - 2 * lax.rem(k, 2)), stations)
+
+    def remote(src, dst, send, recv, device):
+        return pltpu.make_async_remote_copy(
+            src_ref=src, dst_ref=dst, send_sem=send, recv_sem=recv,
+            device_id=device, device_id_type=pl.DeviceIdType.MESH,
+        )
+
+    def chan_copy(g, p, k):
+        peer = lax.rem(mine + g, groups)
+        start = peer * kept + target(k) * share + p * depth
+        return remote(
+            sent_ref.at[pl.ds(start, depth)], arrived.at[g - 1, p, k],
+            chan_send.at[g - 1, p, k], chan_recv.at[g - 1, p, k], (me, peer),
+        )
+
+    def count_copy(g):
+        return remote(
+            count_ref, counts.at[g - 1], count_send.at[g - 1], count_recv.at[g - 1], (me, lax.rem(mine + g, groups))
+        )
+
+    def beam_copy(p, k):
+        return remote(outgoing.at[p, k], gathered.at[p, me], beam_send.at[p, k], beam_recv.at[p, k], (target(k), mine))
+
+    def back_copy(p, k):
+        there = target(k)
+        return remote(
+            sums.at[p, pl.ds(pl.multiple_of(there * beams, beams), beams)],
+            returned.at[p, me], back_send.at[p, k], back_recv.at[p, k], (there, mine),
+        )
+
+    load = pltpu.make_async_copy(own_hbm.at[pl.ds(0, kept)], own, own_sem)
+    load.start()
+    barrier = pltpu.get_barrier_semaphore()
+    for g in range(1, groups):
+        pl.semaphore_signal(
+            barrier, inc=1, device_id=(me, lax.rem(mine + g, groups)), device_id_type=pl.DeviceIdType.MESH
+        )
+
+    @pl.loop(0, stations - 1)
+    def _(k):
+        pl.semaphore_signal(barrier, inc=1, device_id=(target(k), mine), device_id_type=pl.DeviceIdType.MESH)
+
+    pl.semaphore_wait(barrier, groups - 1 + stations - 1)
+
+    for g in range(1, groups):
+        count_copy(g).start()
+    for p in range(phases):
+        @pl.loop(0, stations)
+        def _(k):
+            for g in range(1, groups):
+                chan_copy(g, p, k).start()
+
+    sums[...] = jnp.zeros_like(sums)
+    load.wait()
+    count = count_ref[...]
+    for g in range(1, groups):
+        count_copy(g).wait_recv()
+        count = count + counts[g - 1]
+    gain = lax.rsqrt(count)[0:1, :times].reshape(1, 1, times)
+
+    def chunk(p, k):
+        start = target(k) * share + p * depth
+        total = own[pl.ds(start, depth)]
+        for g in range(1, groups):
+            chan_copy(g, p, k).wait_recv()
+            total = total + arrived[g - 1, p, k].astype(jnp.float32)
+        return (total * gain).astype(jnp.bfloat16)
+
+    def forward(p, k):
+        outgoing[p, k] = chunk(p, k)
+        beam_copy(p, k).start()
+
+    def forward_range(p, first, last, extra=None):
+        @pl.loop(first, last)
+        def _(k):
+            forward(p, k)
+            if extra is not None:
+                extra(k)
+
+    def keep(p):
+        gathered[p, me] = chunk(p, stations - 1)
+
+    def await_beams(p):
+        @pl.loop(0, stations - 1)
+        def _(k):
+            beam_copy(p, k).wait_recv()
+
+    columns = stations * beams
+    lanes = sums.shape[2]
+
+    def correlate(p, index):
+        j, piece = index // pieces, lax.rem(index, pieces)
+
+        def beams_of(stations_slice, count, part):
+            return gathered[p, stations_slice, j, pl.ds(part * beams, beams), :].reshape(count * beams, times)
+
+        some = pl.ds(piece * wide, wide)
+        x_re, x_im = beams_of(some, wide, 0), beams_of(some, wide, 1)
+        every = pl.ds(0, stations)
+        y = jnp.concatenate([beams_of(every, stations, 0), beams_of(every, stations, 1)], axis=1)
+        same = lax.rem(lax.broadcasted_iota(jnp.int32, (wide * beams, columns), 0), beams) == lax.rem(
+            lax.broadcasted_iota(jnp.int32, (wide * beams, columns), 1), beams
+        )
+        station_of = lax.broadcasted_iota(jnp.int32, (columns, lanes), 0) // beams
+        lane = lax.broadcasted_iota(jnp.int32, (columns, lanes), 1)
+        where = pl.ds(pl.multiple_of(piece * (wide * beams), wide * beams), wide * beams)
+        total = sums[p, where, :]
+        for part, x in enumerate((jnp.concatenate([x_re, x_im], axis=1), jnp.concatenate([x_im, -x_re], axis=1))):
+            pairs = lax.dot_general(x, y, (((1,), (1,)), ((), ())), preferred_element_type=jnp.float32)
+            high, low = split(jnp.where(same, pairs, 0.0))
+            place = (lane == station_of + (j * 2 + part) * stations).astype(jnp.float32).astype(jnp.bfloat16)
+            total = total + (
+                jnp.dot(high, place, preferred_element_type=jnp.float32)
+                + jnp.dot(low, place, preferred_element_type=jnp.float32)
+            )
+        sums[p, where, :] = total
+
+    def send_back(p):
+        @pl.loop(0, stations - 1)
+        def _(k):
+            back_copy(p, k).start()
+
+        returned[p, me] = sums[p, pl.ds(pl.multiple_of(me * beams, beams), beams), :]
+
+    last = phases - 1
+    for p in range(phases):
+        if p == 0:
+            forward_range(p, 0, stations - 1)
+        else:
+            quarter, half = stations // 4, stations // 2
+            each = depth * pieces // half
+            forward_range(p, 0, quarter)
+            await_beams(p - 1)
+
+            def extra(k):
+                for c in range(each):
+                    correlate(p - 1, (k - quarter) * each + c)
+
+            forward_range(p, quarter, quarter + half, extra)
+            send_back(p - 1)
+            forward_range(p, quarter + half, stations - 1)
+        keep(p)
+    await_beams(last)
+
+    @pl.loop(0, depth * pieces)
+    def _(index):
+        correlate(last, index)
+
+    send_back(last)
+    for p in range(phases):
+        @pl.loop(0, stations - 1)
+        def _(k):
+            back_copy(p, k).wait_recv()
+    out_ref[...] = returned[...]
+    for g in range(1, groups):
+        count_copy(g).wait_send()
+    for p in range(phases):
+        @pl.loop(0, stations)
+        def _(k):
+            for g in range(1, groups):
+                chan_copy(g, p, k).wait_send()
+
+        @pl.loop(0, stations - 1)
+        def _(k):
+            beam_copy(p, k).wait_send()
+            back_copy(p, k).wait_send()
+
+
+def exchange(sent, own, count, beams, groups, stations):
+    subbands, rows, times = sent.shape
+    kept = subbands // groups
+    share = kept // stations
+    phases = 2 if share % 4 == 0 else 1
+    depth = share // phases
+    lanes = depth * 2 * stations
+    dma = pltpu.SemaphoreType.DMA
+    return pl.pallas_call(
+        exchange_kernel,
+        out_shape=jax.ShapeDtypeStruct((phases, stations, beams, lanes), jnp.float32),
+        in_specs=[
+            pl.BlockSpec(memory_space=pl.ANY),
+            pl.BlockSpec(memory_space=pl.ANY),
+            pl.BlockSpec(memory_space=pltpu.VMEM),
+        ],
+        out_specs=pl.BlockSpec(memory_space=pltpu.VMEM),
+        scratch_shapes=[
+            pltpu.VMEM((kept, rows, times), jnp.float32),
+            pltpu.VMEM((groups - 1, phases, stations, depth, rows, times), jnp.bfloat16),
+            pltpu.VMEM((phases, stations, depth, rows, times), jnp.bfloat16),
+            pltpu.VMEM((phases, stations, depth, rows, times), jnp.bfloat16),
+            pltpu.VMEM((phases, stations * beams, lanes), jnp.float32),
+            pltpu.VMEM((phases, stations, beams, lanes), jnp.float32),
+            pltpu.VMEM((groups - 1, 8, LANES), jnp.float32),
+            dma,
+            dma((groups - 1,)),
+            dma((groups - 1,)),
+            dma((groups - 1, phases, stations)),
+            dma((groups - 1, phases, stations)),
+            dma((phases, stations)),
+            dma((phases, stations)),
+            dma((phases, stations)),
+            dma((phases, stations)),
+        ],
+        compiler_params=pltpu.CompilerParams(
+            collective_id=0, has_side_effects=True, vmem_limit_bytes=40 * 1024 * 1024
+        ),
+    )(sent, own, count)
+
+
 def on_device(samples, weights, antenna_flags, subband_table):
     usable = antenna_flags.astype(jnp.float32)
-    usable_count = lax.psum(jnp.sum(usable, axis=1), "chan")
-    gain_scale = lax.rsqrt(usable_count)
-    groups = lax.axis_size("chan")
-    mine = lax.axis_index("chan")
-    beams, times = weights.shape[2], samples.shape[3]
+    groups, stations = lax.axis_size("chan"), lax.axis_size("station")
+    beams = weights.shape[2]
     sent, own = beam_partials(samples, weights, usable, subband_table, groups)
-    sent = sent.reshape(groups, -1, 2, beams, times)
-    arrived = lax.all_to_all(sent, "chan", 0, 0)
-    own = own[:-1].reshape(-1, 2, beams, times)
-    is_mine = (jnp.arange(groups) == mine)[:, None, None, None, None]
-    beam_sum = own + jnp.sum(jnp.where(is_mine, 0.0, arrived.astype(jnp.float32)), axis=0)
-    beam_data = (beam_sum * gain_scale).astype(jnp.bfloat16)
-    stations = lax.axis_size("station")
-    spread = beam_data.reshape(stations, -1, *beam_data.shape[1:])
-    gathered = lax.all_to_all(spread, "station", 0, 0)
-    swapped = jnp.stack([gathered[:, :, 1], -gathered[:, :, 0]], axis=2)
-    stacked = jnp.stack([gathered, swapped], axis=0)
-    pairs = jnp.einsum("osfcbt,rfcbt->sfobr", stacked, gathered, preferred_element_type=jnp.float32)
-    returned = lax.all_to_all(pairs, "station", 0, 0)
-    return returned.reshape(-1, *returned.shape[2:])[:, :, None]
+    count = jnp.broadcast_to(jnp.sum(usable, axis=1)[:, None], (8, LANES))
+    back = exchange(sent, own, count, beams, groups, stations)
+    phases = back.shape[0]
+    back = back.reshape(phases, stations, beams, -1, 2, stations)
+    back = back.transpose(1, 0, 3, 4, 2, 5)
+    return back.reshape(-1, 2, 1, beams, stations)
 
 
 def solution(mesh):

time: 204 us -> 131 us (0.64)
  blocking collectives: 121 us -> 0 us
  Pallas kernels: 41.8 us -> 121 us
  local copies, waits for them, and re-layouts: 18.2 us -> 7.73 us
  other arithmetic: 9.48 us -> 2.42 us
  matrix products: 6.47 us -> 0 us
  starting transfers between devices: 5.72 us -> 0 us
    pallas_call x0 -> x1, Pallas kernels: none -> 79 us  [exchange(): pl.pallas_call(exchange_kernel, out_shape=jax.ShapeDtypeStruct((phases, s...]
    all_to_all x2 -> x0, blocking collectives: 72.3 us -> none  [the longest x1 53.1 us: on_device(): gathered = lax.all_to_all(spread, 'station', 0, 0)]
    psum x1 -> x0, blocking collectives: 48.9 us -> none  [on_device(): usable_count = lax.psum(jnp.sum(usable, axis=1), 'chan')]
    dot_general x1 -> x0, matrix products: 6.47 us -> none  [on_device(): jnp.einsum('osfcbt,rfcbt->sfobr', stacked, gathered, preferred_element_ty...]
    all_to_all x1 -> x0, starting transfers between devices: 5.72 us -> none  [on_device(): arrived = lax.all_to_all(sent, 'chan', 0, 0)]
    slice x1 -> x0, local copies, waits for them, and re-layouts: 4.72 us -> none  [on_device(): own = own[:-1].reshape(-1, 2, beams, times)]
    reduce_sum x2 -> x1, other arithmetic: 4.93 us -> 1.25 us  [on_device(): count = jnp.broadcast_to(jnp.sum(usable, axis=1)[:, None], (8, LANES))]
    transpose x1, local copies, waits for them, and re-layouts: 4.28 us -> 0.6 us  [on_device(): back = back.transpose(1, 0, 3, 4, 2, 5)]
  transfers between devices with their start and end apart: 1 -> 0, of which waited for: 0 -> 0; matrix products, arithmetic and copies ran while one was open for 3% -> 0% of each run, Pallas kernels for 0% -> 0%
where the time goes in v1:
time: 131 us
  Pallas kernels  121 us (92%)
  local copies, waits for them, and re-layouts  7.73 us (6%)
  other arithmetic  2.42 us (2%)
    pallas_call x1, Pallas kernels, exchange(): pl.pallas_call(exchange_kernel, out_shape=jax.ShapeDtypeStruct((phases, s...  79 us
    pallas_call x1, Pallas kernels, beam_partials(): pl.pallas_call(functools.partial(beam_kernel, antennas=antennas, beams=be...  41.8 us
    unnamed x4, local copies, waits for them, and re-layouts  4.38 us

profile of v1, /device:TPU:0, one launch (start us, length us, event | category | flops | bytes accessed | tf_op | source)
XLA Modules:
  0.0 130.9 jit_solution(866753692915183708)
XLA Ops:
  0.0 1.3 convert_reduce_fusion
  1.3 1.2 convert_element_type.3.usable_ref
  2.4 0.6 broadcast_in_dim.2.count_ref
  3.0 41.8 %shard_map.46 = (bf16[256,64,128]{2,1,0:T(8,128)(2,1)}, f32[129,64,128]{2,1,0:T(8,128)}) custom-call(s32[256]{0:T(256)} %table_ref.1, f32[2,1,128,128,256]{4,3,2,1,0:T(8,128)} %x_ref.1, f32[2,1,32,128,256]{4,3,2,1,0:T(8,128)} %w_ref.1, f32[1,128]{1,0:T(1,128)} %convert_element_type.3.usable_ref), custom_call_target="tpu_custom_call" | custom-call | tf_op jit(solution)/shard_map/pallas_call | solution.py:99
  44.8 0.0 copy-start
  44.8 2.2 %copy-done = f32[129,64,128]{2,1,0:T(8,128)S(1)} copy-done((f32[129,64,128]{2,1,0:T(8,128)S(1)}, f32[129,64,128]{2,1,0:T(8,128)}, u32[]{:S(2)}) %copy-start) | copy-done | bytes 4227096
  47.0 0.0 copy-start.1
  47.0 2.2 %copy-done.1 = bf16[256,64,128]{2,1,0:T(8,128)(2,1)S(1)} copy-done((bf16[256,64,128]{2,1,0:T(8,128)(2,1)S(1)}, bf16[256,64,128]{2,1,0:T(8,128)(2,1)}, u32[]{:S(2)}) %copy-start.1) | copy-done | bytes 4194328
  49.2 79.0 %shard_map.47 = f32[2,16,32,128]{3,2,1,0:T(8,128)S(1)} custom-call(bf16[256,64,128]{2,1,0:T(8,128)(2,1)S(1)} %copy-done.1, f32[129,64,128]{2,1,0:T(8,128)S(1)} %copy-done, f32[8,128]{1,0:T(8,128)S(1)} %broadcast_in_dim.2.count_ref), custom_call_target="tpu_custom_call" | custom-call | tf_op jit(solution)/shard_map/pallas_call | solution.py:304
  128.1 0.6 copy.9
  128.7 2.2 %copy.8 = f32[128,2,1,32,16]{0,4,3,2,1:T(8,128)} copy(f32[128,2,1,32,16]{3,4,1,0,2:T(8,128)S(1)} %bitcast.5) | data formatting | bytes 1048576 | tf_op jit(solution)/shard_map/reshape | solution.py:347
Async XLA Ops:
  44.8 2.2 %copy-start = (f32[129,64,128]{2,1,0:T(8,128)S(1)}, f32[129,64,128]{2,1,0:T(8,128)}, u32[]{:S(2)}) copy-start(f32[129,64,128]{2,1,0:T(8,128)} %get-tuple-element.8.own_hbm) | copy-start | bytes 12681220
  47.0 2.2 %copy-start.1 = (bf16[256,64,128]{2,1,0:T(8,128)(2,1)S(1)}, bf16[256,64,128]{2,1,0:T(8,128)(2,1)}, u32[]{:S(2)}) copy-start(bf16[256,64,128]{2,1,0:T(8,128)(2,1)} %get-tuple-element.7.sent_ref) | copy-start | bytes 12582916

commit v2 on v1

--- a/solution.py
+++ b/solution.py
@@ -8,8 +8,8 @@
 from jax.sharding import PartitionSpec as P
 
 LANES = 128
-ANTENNAS_PER_STEP = 16
-UNROLL = 4
+ANTENNAS_PER_STEP = 32
+UNROLL = 8
 STATIONS_PER_STEP = 4
 
 
@@ -329,7 +329,7 @@
             dma((phases, stations)),
         ],
         compiler_params=pltpu.CompilerParams(
-            collective_id=0, has_side_effects=True, vmem_limit_bytes=40 * 1024 * 1024
+            collective_id=0, has_side_effects=True, vmem_limit_bytes=62 * 1024 * 1024
         ),
     )(sent, own, count)
 

time: 131 us -> 120 us (0.916)
  Pallas kernels: 121 us -> 112 us
  local copies, waits for them, and re-layouts: 7.73 us -> 5.11 us
    pallas_call x1, Pallas kernels: 41.8 us -> 32.1 us  [beam_partials(): pl.pallas_call(functools.partial(beam_kernel, antennas=antennas, beams=be...]
    unnamed x4 -> x0, local copies, waits for them, and re-layouts: 4.38 us -> none
where the time goes in v2:
time: 120 us
  Pallas kernels  112 us (93%)
  local copies, waits for them, and re-layouts  5.11 us (4%)
  other arithmetic  2.51 us (2%)
    pallas_call x1, Pallas kernels, exchange(): pl.pallas_call(exchange_kernel, out_shape=jax.ShapeDtypeStruct((phases, s...  80.2 us
    pallas_call x1, Pallas kernels, beam_partials(): pl.pallas_call(functools.partial(beam_kernel, antennas=antennas, beams=be...  32.1 us

profile of v2, /device:TPU:0, one launch (start us, length us, event | category | flops | bytes accessed | tf_op | source)
XLA Modules:
  0.0 119.9 jit_solution(16673984818898039512)
XLA Ops:
  0.0 1.3 %convert_reduce_fusion = f32[]{:T(128)} fusion(s32[1,128]{1,0:T(1,128)} %param.6), kind=kLoop, calls=%fused_computation | loop fusion | flops 255 | bytes 516 | tf_op jit(solution)/shard_map/reduce_sum | solution.py:342
  1.3 1.2 convert_element_type.3.usable_ref
  2.5 1.3 %broadcast_in_dim.2.count_ref = f32[8,128]{1,0:T(8,128)} broadcast(f32[]{:T(128)} %convert_reduce_fusion), dimensions={} | broadcast | bytes 4100 | tf_op jit(solution)/shard_map/broadcast_in_dim | solution.py:342
  3.8 32.1 %shard_map.46 = (bf16[256,64,128]{2,1,0:T(8,128)(2,1)}, f32[129,64,128]{2,1,0:T(8,128)}) custom-call(s32[256]{0:T(256)} %table_ref.1, f32[2,1,128,128,256]{4,3,2,1,0:T(8,128)} %x_ref.1, f32[2,1,32,128,256]{4,3,2,1,0:T(8,128)} %w_ref.1, f32[1,128]{1,0:T(1,128)} %convert_element_type.3.usable_ref), custom_call_target="tpu_custom_call" | custom-call | tf_op jit(solution)/shard_map/pallas_call | solution.py:99
  35.9 80.2 %shard_map.47 = f32[2,16,32,128]{3,2,1,0:T(8,128)} custom-call(bf16[256,64,128]{2,1,0:T(8,128)(2,1)} %get-tuple-element.7.sent_ref, f32[129,64,128]{2,1,0:T(8,128)} %get-tuple-element.8.own_hbm, f32[8,128]{1,0:T(8,128)} %broadcast_in_dim.2.count_ref), custom_call_target="tpu_custom_call" | custom-call | tf_op jit(solution)/shard_map/pallas_call | solution.py:304
  116.1 1.6 %copy.9 = f32[2,16,32,128]{2,3,0,1:T(8,128)S(1)} copy(f32[2,16,32,128]{3,2,1,0:T(8,128)} %shard_map.47) | data formatting | bytes 1048576 | tf_op jit(solution)/shard_map/transpose | solution.py:346
  117.8 2.2 %copy.8 = f32[128,2,1,32,16]{0,4,3,2,1:T(8,128)} copy(f32[128,2,1,32,16]{3,4,1,0,2:T(8,128)S(1)} %bitcast.5) | data formatting | bytes 1048576 | tf_op jit(solution)/shard_map/reshape | solution.py:347
